TPU v7x, 128 devices: a whole 4x4x4 slice. The times are simulated.
128 devices in a mesh: expert: 16 (over y, x_hi, core), dp: 8 (over x_lo, z).
Axes of the slice: x: 4 (x_hi: 2, x_lo: 2; x = x_hi * 2 + x_lo), y: 4, z: 4, core: 2. Of those that a mesh axis runs over, the one named last changes fastest.
Arguments:
- gradient: bfloat16 [8, 1, 14336, 2048], P('dp', None, None, 'expert'), may hold values from -6 to 6
- momentum: float32 [8, 1, 14336, 2048], P('dp', None, 'expert'), may hold values from -6 to 6
- group_index: int32 [224, 32, 8, 32], P('expert'), may hold values from 0 to 4095, all different within a row
Outputs:
- momentum_next: float32 [8, 1, 14336, 2048], P('dp', None, 'expert')
- update: float32 [1, 14336, 2048], P(None, None, 'expert')
Inputs may be any that keep to these rules, and one draw needn't show every extreme that they name: `group_index`: an entry names the coefficient at row frequency (entry // 64) and column frequency (entry % 64) of its block; the 32 entries of one block and replica differ.
All inputs are finite; a program needn't handle non-finite values.
Results may differ from a plain program's by a relative error of at most 0.0003.
Values may be sent and summed in bfloat16 or wider, within the bound.
A program may use at most 192 MiB of HBM per device.

v0:
```python
import math
import jax
import jax.numpy as jnp
from jax import lax
from jax.sharding import PartitionSpec as P

SPAN = 64
MOMENTUM_DECAY = 0.999
HIGHEST_PRECISION = lax.Precision.HIGHEST


def in_blocks(x, dim, count):
    before, after = (x.shape[:dim], x.shape[dim + 1 :])
    return jnp.moveaxis(x.reshape(*before, count, -1, *after), dim, 0)


def edges_of(length, count):
    unit = 8 if length >= 8 * count else 1
    return [length // unit * k // count * unit for k in range(1, count)]


def in_order(tiles, dim):
    shape = list(tiles.shape[1:])
    shape[dim] *= tiles.shape[0]
    return jnp.moveaxis(tiles, 0, dim).reshape(shape)


def several_exchanges(x, axis, pieces, split_dim, concat_dim):
    tiles = in_blocks(x, split_dim, lax.axis_size(axis))
    split_at = max(range(1, max(2, tiles.ndim - 1)), key=lambda d: tiles.shape[d])
    outs = []
    for piece in jnp.split(tiles, edges_of(tiles.shape[split_at], pieces), axis=split_at):
        if piece.size:
            outs.append(lax.all_to_all(piece, axis, split_axis=0, concat_axis=0, tiled=True))
    return in_order(jnp.concatenate(outs, axis=split_at), concat_dim)


def cosine_table(order_size):
    frequency = jnp.arange(order_size, dtype=jnp.float32)[:, None]
    position = jnp.arange(order_size, dtype=jnp.float32)[None, :]
    weighting = jnp.where(frequency == 0, math.sqrt(1.0 / order_size), math.sqrt(2.0 / order_size))
    return weighting * jnp.cos(math.pi * (2.0 * position + 1.0) * frequency / (2.0 * order_size))


def forward(blocks, cosine):
    return jnp.einsum("ui,piqj,vj->pquv", cosine, blocks, cosine, precision=HIGHEST_PRECISION)


def inverse(coeffs, cosine):
    return jnp.einsum("ui,pquv,vj->piqj", cosine, coeffs, cosine, precision=HIGHEST_PRECISION)


def place(values, picked, total):
    count_rows = picked.shape[0]
    count_cols = picked.shape[1]
    row_ids = jnp.arange(count_rows, dtype=jnp.int32)[:, None, None]
    col_ids = jnp.arange(count_cols, dtype=jnp.int32)[None, :, None]
    empty = jnp.zeros((count_rows, count_cols, total), jnp.float32)
    return empty.at[row_ids, col_ids, picked].add(values)


def on_device(gradient, momentum, group_index):
    cosine = cosine_table(SPAN)
    replica = lax.axis_index("dp")
    shifted = several_exchanges(gradient, "expert", 2, 2, 3)
    row_count = shifted.shape[1] * shifted.shape[2]
    col_count = shifted.shape[3]
    decayed = MOMENTUM_DECAY * momentum.reshape(row_count, col_count) + shifted.reshape(
        row_count, col_count
    ).astype(jnp.float32)
    block_rows = row_count // SPAN
    block_cols = col_count // SPAN
    blocks = decayed.reshape(block_rows, SPAN, block_cols, SPAN)
    coeffs = forward(blocks, cosine).reshape(block_rows, block_cols, SPAN * SPAN)
    own = lax.dynamic_index_in_dim(group_index, replica, 2, keepdims=False)
    values = jnp.take_along_axis(coeffs, own, axis=2)
    selected = place(values, own, SPAN * SPAN).reshape(block_rows, block_cols, SPAN, SPAN)
    restored = inverse(selected, cosine).reshape(row_count, col_count)
    momentum_next = (decayed - restored).reshape(momentum.shape)
    total = lax.psum(restored, "dp")
    update = several_exchanges(total[None], "expert", 2, 2, 1)
    return (momentum_next, update)


def solution(mesh):
    placed = (
        P("dp", None, None, "expert"),
        P("dp", None, "expert", None),
        P("expert", None, None, None),
    )
    return jax.shard_map(
        on_device,
        mesh=mesh,
        in_specs=placed,
        out_specs=(P("dp", None, "expert", None), P(None, None, "expert")),
        check_vma=False,
    )
```

profile of v0, /device:TPU:1, one launch (start us, length us, event | category | flops | bytes accessed | tf_op | source)
XLA Modules:
  0.0 818.0 jit_solution(18265335012599855802)
XLA Ops:
  7.2 4.3 fusion.28
  11.5 8.4 %all-to-all-start = ((bf16[16,1,1,448,128]{4,3,2,1,0:T(8,128)(2,1)}), bf16[16,1,1,448,128]{4,3,2,1,0:T(8,128)(2,1)}, u32[]{:S(2)}, u32[]{:S(2)}) async-start(bf16[16,1,1,448,128]{4,3,2,1,0:T(8,128)(2,1)} %get-tuple-element.6), calls=%async_computation | async-start | bytes 3670016 | tf_op jit(solution)/shard_map/all_to_all | solution.py:34
  19.9 25.6 %all-to-all-done = bf16[16,1,1,448,128]{4,3,2,1,0:T(8,128)(2,1)} async-done(((bf16[16,1,1,448,128]{4,3,2,1,0:T(8,128)(2,1)}), bf16[16,1,1,448,128]{4,3,2,1,0:T(8,128)(2,1)}, u32[]{:S(2)}, u32[]{:S(2)}) %all-to-all-start) | async-done | bytes 1835040 | tf_op jit(solution)/shard_map/all_to_all | solution.py:34
  45.5 5.2 all-to-all-start.1
  50.8 7.7 broadcast_multiply_fusion
  58.5 12.7 %mul.98 = f32[14,64,32,64]{3,2,1,0:T(8,128)} reshape(f32[1,1,896,2048]{3,2,1,0:T(8,128)} %broadcast_multiply_fusion) | data formatting | bytes 14680064 | tf_op jit(solution)/shard_map/mul | solution.py:68
  72.2 4.2 all-to-all-done.1
  76.5 6.1 convert_bitcast_fusion
  82.5 7.3 copy.28
  89.8 11.4 %reshape.106 = f32[14,64,32,64]{3,2,1,0:T(8,128)} reshape(f32[1,1,896,16,128]{4,3,2,1,0:T(8,128)} %copy.28) | data formatting | bytes 14680064 | tf_op jit(solution)/shard_map/convert_element_type | solution.py:70
  101.2 15.0 %add.64 = f32[14,64,32,64]{3,2,1,0:T(8,128)} add(f32[14,64,32,64]{3,2,1,0:T(8,128)} %mul.98, f32[14,64,32,64]{3,2,1,0:T(8,128)} %reshape.106) | non-fusion elementwise | flops 1835008 | bytes 22020096 | tf_op jit(solution)/shard_map/add | solution.py:68
  116.2 27.7 %fusion = f32[14,32,64,64]{2,3,1,0:T(8,128)S(1)} fusion(f32[14,64,32,64]{3,2,1,0:T(8,128)} %add.64, f32[64]{0:T(128)S(1)} %get-tuple-element.11, f32[64]{0:T(128)S(1)} %get-tuple-element.10), kind=kOutput, calls=%fused_computation.2 | convolution fusion | flops 1409298432 | bytes 14680576 | tf_op jit(solution)/shard_map/ui,piqj,vj->pquv/dot_general | solution.py:46
  143.9 14.9 %fusion.8 = f32[14,32,64,64]{3,2,1,0:T(8,128)} fusion(f32[14,32,64,64]{2,3,1,0:T(8,128)S(1)} %fusion, f32[64]{0:T(128)S(1)} %get-tuple-element.11, f32[64]{0:T(128)S(1)} %get-tuple-element.10), kind=kOutput, calls=%fused_computation.25 | convolution fusion | flops 1409298432 | bytes 14680576 | tf_op jit(solution)/shard_map/ui,piqj,vj->pquv/dot_general | solution.py:46
  158.8 12.9 %reshape.95 = f32[14,32,4096]{2,1,0:T(8,128)} reshape(f32[14,32,64,64]{3,2,1,0:T(8,128)} %fusion.8) | data formatting | bytes 14680064 | tf_op jit(solution)/shard_map/reshape | solution.py:74
  171.7 199.1 %gather_fusion = f32[14336]{0:T(1024)S(1)} fusion(f32[14,32,4096]{2,1,0:T(8,128)} %reshape.95, s32[14336]{0:T(1024)S(1)} %reshape.107), kind=kCustom, calls=%fused_computation | custom fusion | bytes 286720 | tf_op jit(solution)/shard_map/jit(take_along_axis)/gather | solution.py:76
  371.1 78.6 %scatter_custom_fusion = f32[1835008]{0:T(1024)} fusion(s32[14336]{0:T(1024)S(1)} %reshape.113, f32[14336]{0:T(1024)S(1)} %reshape.115, f32[]{:T(128)} %constant.15.clone.1), kind=kCustom, calls=%fused_computation.11 | custom fusion | flops 14336 | bytes 7340036
  449.7 11.5 %reshape.96 = f32[14,32,64,64]{3,2,1,0:T(8,128)} reshape(f32[1835008]{0:T(1024)} %scatter_custom_fusion) | data formatting | bytes 14680064 | tf_op jit(solution)/shard_map/reshape | solution.py:77
  461.2 18.2 %fusion.6 = f32[14,32,64,64]{2,3,1,0:T(8,128)S(1)} fusion(f32[14,32,64,64]{3,2,1,0:T(8,128)} %reshape.96, f32[64]{0:T(128)S(1)} %get-tuple-element.11, f32[64]{0:T(128)S(1)} %get-tuple-element.10), kind=kOutput, calls=%fused_computation.23 | convolution fusion | flops 1409298432 | bytes 14680576 | tf_op jit(solution)/shard_map/ui,pquv,vj->piqj/dot_general | solution.py:50
  479.4 14.7 %convolution_bitcast_fusion = f32[14,64,32,64]{3,1,2,0:T(8,128)} fusion(f32[14,32,64,64]{2,3,1,0:T(8,128)S(1)} %fusion.6, f32[64]{0:T(128)S(1)} %get-tuple-element.11, f32[64]{0:T(128)S(1)} %get-tuple-element.10), kind=kOutput, calls=%fused_computation.6 | convolution fusion | flops 1409298432 | bytes 14680576 | tf_op jit(solution)/shard_map/ui,pquv,vj->piqj/dot_general | solution.py:50
  494.1 21.3 %copy.34 = f32[14,64,32,64]{3,2,1,0:T(8,128)} copy(f32[14,64,32,64]{3,1,2,0:T(8,128)} %convolution_bitcast_fusion) | data formatting | bytes 14680064 | tf_op jit(solution)/shard_map/ui,pquv,vj->piqj/transpose | solution.py:50
  515.4 12.8 %reshape_broadcast_in_dim.3 = f32[1,896,16,128]{3,2,1,0:T(8,128)} reshape(f32[14,64,32,64]{3,2,1,0:T(8,128)} %copy.34) | data formatting | bytes 14680064 | tf_op jit(solution)/shard_map/reshape;broadcast_in_dim | solution.py:14
  528.2 163.8 %all-reduce.2.cloned.1.call-done = f32[16,1,896,128]{3,0,2,1:T(8,128)} async-done(((f32[16,1,896,128]{3,0,2,1:T(8,128)}), f32[16,1,896,128]{3,0,2,1:T(8,128)}) %all-reduce.2.cloned.1.call-update) | async-done | bytes 7340048 | tf_op jit(solution)/shard_map/psum | solution.py:80
  692.0 5.5 fusion.27
  697.5 2.9 copy.36
  700.4 7.3 all-to-all-start.2
  707.7 5.1 copy.37
  712.8 40.2 %all-to-all-done.2 = f32[16,1,448,128]{3,2,1,0:T(8,128)} async-done(((f32[16,1,448,128]{3,2,1,0:T(8,128)}), f32[16,1,448,128]{3,2,1,0:T(8,128)}, u32[]{:S(2)}, u32[]{:S(2)}) %all-to-all-start.2) | async-done | bytes 3670048 | tf_op jit(solution)/shard_map/all_to_all | solution.py:34
  753.0 5.3 all-to-all-start.3
  758.2 13.2 %reshape.97 = f32[1,1,896,2048]{3,2,1,0:T(8,128)} reshape(f32[14,64,32,64]{3,2,1,0:T(8,128)} %copy.34) | data formatting | bytes 14680064 | tf_op jit(solution)/shard_map/reshape | solution.py:78
  771.5 13.0 %fusion.2 = f32[1,1,896,2048]{3,2,1,0:T(8,128)} fusion(f32[1,1,896,2048]{3,2,1,0:T(8,128)} %reshape.97, f32[16,1,1,112,8,128]{5,4,3,2,1,0:T(8,128)} %get-tuple-element.4, f32[1,1,896,2048]{3,2,1,0:T(8,128)} %param.4), kind=kLoop, calls=%fused_computation.8 | loop fusion | flops 5505024 | bytes 29360128 | tf_op jit(solution)/shard_map/sub | solution.py:79
  784.5 19.2 %all-to-all-done.3 = f32[16,1,448,128]{3,2,1,0:T(8,128)} async-done(((f32[16,1,448,128]{3,2,1,0:T(8,128)}), f32[16,1,448,128]{3,2,1,0:T(8,128)}, u32[]{:S(2)}, u32[]{:S(2)}) %all-to-all-start.3) | async-done | bytes 3670048 | tf_op jit(solution)/shard_map/all_to_all | solution.py:34
  803.6 7.0 pad_maximum_fusion
  (23 shorter events, 1.3 us)
Async XLA Ops:
  7.2 64.0 %copy-start = (s32[14,32,8,32]{3,2,1,0:T(8,128)S(1)}, s32[14,32,8,32]{3,2,1,0:T(8,128)}, u32[]{:S(2)}) copy-start(s32[14,32,8,32]{3,2,1,0:T(8,128)} %param.5) | copy-start | bytes 1376260
  11.5 34.1 %all-to-all-start = ((bf16[16,1,1,448,128]{4,3,2,1,0:T(8,128)(2,1)}), bf16[16,1,1,448,128]{4,3,2,1,0:T(8,128)(2,1)}, u32[]{:S(2)}, u32[]{:S(2)}) async-start(bf16[16,1,1,448,128]{4,3,2,1,0:T(8,128)(2,1)} %get-tuple-element.6), calls=%async_computation | async-start | bytes 3670016 | tf_op jit(solution)/shard_map/all_to_all | solution.py:34
  45.5 30.9 %all-to-all-start.1 = ((bf16[16,1,1,448,128]{4,3,2,1,0:T(8,128)(2,1)}), bf16[16,1,1,448,128]{4,3,2,1,0:T(8,128)(2,1)}, u32[]{:S(2)}, u32[]{:S(2)}) async-start(bf16[16,1,1,448,128]{4,3,2,1,0:T(8,128)(2,1)} %get-tuple-element.7), calls=%async_computation.1 | async-start | bytes 3670016 | tf_op jit(solution)/shard_map/all_to_all | solution.py:34
  50.7 641.3 %all-reduce.2.cloned.1.call-start = ((), (), s32[]{:S(2)}) async-start(), calls=%async_computation.4 | async-start | bytes 14680064 | tf_op jit(solution)/shard_map/psum | solution.py:80
  58.5 13.2 %copy-start.3 = (s32[3]{0:T(128)S(1)}, s32[3]{0:T(128)}, u32[]{:S(2)}) copy-start(s32[3]{0:T(128)} %constant.54) | copy-start | bytes 40
  58.5 13.3 %copy-start.2 = (s32[3]{0:T(128)S(1)}, s32[3]{0:T(128)}, u32[]{:S(2)}) copy-start(s32[3]{0:T(128)} %constant.57) | copy-start | bytes 40
  700.4 52.6 %all-to-all-start.2 = ((f32[16,1,448,128]{3,2,1,0:T(8,128)}), f32[16,1,448,128]{3,2,1,0:T(8,128)}, u32[]{:S(2)}, u32[]{:S(2)}) async-start(f32[16,1,448,128]{3,2,1,0:T(8,128)} %copy.36), calls=%async_computation.2 | async-start | bytes 7340032 | tf_op jit(solution)/shard_map/all_to_all | solution.py:34
  753.0 50.7 %all-to-all-start.3 = ((f32[16,1,448,128]{3,2,1,0:T(8,128)}), f32[16,1,448,128]{3,2,1,0:T(8,128)}, u32[]{:S(2)}, u32[]{:S(2)}) async-start(f32[16,1,448,128]{3,2,1,0:T(8,128)} %copy.37), calls=%async_computation.3 | async-start | bytes 7340032 | tf_op jit(solution)/shard_map/all_to_all | solution.py:34
  803.6 7.0 copy-start.1
Sparse Core Ops, SparseCore 0:
  528.4 163.5 all-reduce.1
where the time goes:
time: 834 us; the launch traced here: 818 us
  local copies, waits for them, and re-layouts  321 us (38%)
  waiting for transfers between devices  253 us (30%)
  other arithmetic  128 us (15%)
  matrix products  75.5 us (9%)
  starting transfers between devices  26.2 us (3%)
  between operations  14.6 us (2%)
    gather x2, local copies, waits for them, and re-layouts, on_device(): values = jnp.take_along_axis(coeffs, own, axis=2)  199 us
    psum x1, waiting for transfers between devices, on_device(): total = lax.psum(restored, 'dp')  164 us
    all_to_all x4, waiting for transfers between devices, several_exchanges(): lax.all_to_all(piece, axis, split_axis=0, concat_axis=0, tiled=True)  89.3 us
    unnamed x5, other arithmetic  85.1 us
    dot_general x2, matrix products, forward(): jnp.einsum('ui,piqj,vj->pquv', cosine, blocks, cosine, precision=HIGHEST_...  42.6 us
    dot_general x2, matrix products, inverse(): jnp.einsum('ui,pquv,vj->piqj', cosine, coeffs, cosine, precision=HIGHEST_...  32.9 us
    all_to_all x4, starting transfers between devices, several_exchanges(): lax.all_to_all(piece, axis, split_axis=0, concat_axis=0, tiled=True)  26.1 us
    transpose x1, local copies, waits for them, and re-layouts, inverse(): jnp.einsum('ui,pquv,vj->piqj', cosine, coeffs, cosine, precision=HIGHEST_...  21.3 us
  transfers between devices with their start and end apart: 5, of which 5 were waited for; matrix products, arithmetic and copies ran while one was open for 6% of the time, Pallas kernels for 0%

commit v1 on v0

--- a/solution.py
+++ b/solution.py
@@ -77,7 +77,7 @@
     selected = place(values, own, SPAN * SPAN).reshape(block_rows, block_cols, SPAN, SPAN)
     restored = inverse(selected, cosine).reshape(row_count, col_count)
     momentum_next = (decayed - restored).reshape(momentum.shape)
-    total = lax.psum(restored, "dp")
+    total = lax.all_gather(restored, "dp").sum(axis=0)
     update = several_exchanges(total[None], "expert", 2, 2, 1)
     return (momentum_next, update)
 

time: 834 us -> 1270 us (1.52)
  waiting for transfers between devices: 253 us -> 652 us
  other arithmetic: 128 us -> 150 us
  local copies, waits for them, and re-layouts: 321 us -> 335 us
    all_gather x0 -> x1, waiting for transfers between devices: none -> 563 us  [on_device(): total = lax.all_gather(restored, 'dp').sum(axis=0)]
    psum x1 -> x0, waiting for transfers between devices: 164 us -> none  [on_device(): total = lax.psum(restored, 'dp')]
    reduce_sum x0 -> x1, other arithmetic: none -> 21.8 us  [on_device(): total = lax.all_gather(restored, 'dp').sum(axis=0)]
  transfers between devices with their start and end apart: 5 -> 5, of which waited for: 5 -> 5; matrix products, arithmetic and copies ran while one was open for 6% -> 4% of each run, Pallas kernels for 0% -> 0%
where the time goes in v1:
time: 1270 us; the launch traced here: 1250 us
  waiting for transfers between devices  652 us (51%)
  local copies, waits for them, and re-layouts  335 us (26%)
  other arithmetic  150 us (12%)
  matrix products  75.4 us (6%)
  starting transfers between devices  26.2 us (2%)
  between operations  14.7 us (1%)
    all_gather x1, waiting for transfers between devices, on_device(): total = lax.all_gather(restored, 'dp').sum(axis=0)  563 us
    gather x2, local copies, waits for them, and re-layouts, on_device(): values = jnp.take_along_axis(coeffs, own, axis=2)  199 us
    all_to_all x4, waiting for transfers between devices, several_exchanges(): lax.all_to_all(piece, axis, split_axis=0, concat_axis=0, tiled=True)  89.1 us
    unnamed x5, other arithmetic  85.1 us
    dot_general x2, matrix products, forward(): jnp.einsum('ui,piqj,vj->pquv', cosine, blocks, cosine, precision=HIGHEST_...  42.6 us
    dot_general x2, matrix products, inverse(): jnp.einsum('ui,pquv,vj->piqj', cosine, coeffs, cosine, precision=HIGHEST_...  32.8 us
    all_to_all x4, starting transfers between devices, several_exchanges(): lax.all_to_all(piece, axis, split_axis=0, concat_axis=0, tiled=True)  26.1 us
  transfers between devices with their start and end apart: 5, of which 5 were waited for; matrix products, arithmetic and copies ran while one was open for 4% of the time, Pallas kernels for 0%

profile of v1, /device:TPU:1, one launch (start us, length us, event | category | flops | bytes accessed | tf_op | source)
XLA Modules:
  0.0 1253.3 jit_solution(15264112155570038276)
XLA Ops:
  11.5 8.4 all-to-all-start
  19.9 25.6 %all-to-all-done = bf16[16,1,1,448,128]{4,3,2,1,0:T(8,128)(2,1)} async-done(((bf16[16,1,1,448,128]{4,3,2,1,0:T(8,128)(2,1)}), bf16[16,1,1,448,128]{4,3,2,1,0:T(8,128)(2,1)}, u32[]{:S(2)}, u32[]{:S(2)}) %all-to-all-start) | async-done | bytes 1835040 | tf_op jit(solution)/shard_map/all_to_all | solution.py:34
  45.5 5.2 all-to-all-start.1
  51.8 7.7 broadcast_multiply_fusion
  59.5 12.7 %mul.98 = f32[14,64,32,64]{3,2,1,0:T(8,128)} reshape(f32[1,1,896,2048]{3,2,1,0:T(8,128)} %broadcast_multiply_fusion) | data formatting | bytes 14680064 | tf_op jit(solution)/shard_map/mul | solution.py:68
  76.5 6.1 convert_bitcast_fusion
  82.5 7.3 copy.28
  89.8 11.4 reshape.102
  101.2 15.0 %add.62 = f32[14,64,32,64]{3,2,1,0:T(8,128)} add(f32[14,64,32,64]{3,2,1,0:T(8,128)} %mul.98, f32[14,64,32,64]{3,2,1,0:T(8,128)} %reshape.102) | non-fusion elementwise | flops 1835008 | bytes 22020096 | tf_op jit(solution)/shard_map/add | solution.py:68
  116.2 27.7 %fusion = f32[14,32,64,64]{2,3,1,0:T(8,128)S(1)} fusion(f32[14,64,32,64]{3,2,1,0:T(8,128)} %add.62, f32[64]{0:T(128)S(1)} %get-tuple-element.11, f32[64]{0:T(128)S(1)} %get-tuple-element.10), kind=kOutput, calls=%fused_computation.2 | convolution fusion | flops 1409298432 | bytes 14680576 | tf_op jit(solution)/shard_map/ui,piqj,vj->pquv/dot_general | solution.py:46
  144.0 14.9 %fusion.8 = f32[14,32,64,64]{3,2,1,0:T(8,128)} fusion(f32[14,32,64,64]{2,3,1,0:T(8,128)S(1)} %fusion, f32[64]{0:T(128)S(1)} %get-tuple-element.11, f32[64]{0:T(128)S(1)} %get-tuple-element.10), kind=kOutput, calls=%fused_computation.25 | convolution fusion | flops 1409298432 | bytes 14680576 | tf_op jit(solution)/shard_map/ui,piqj,vj->pquv/dot_general | solution.py:46
  158.8 12.9 %reshape.93 = f32[14,32,4096]{2,1,0:T(8,128)} reshape(f32[14,32,64,64]{3,2,1,0:T(8,128)} %fusion.8) | data formatting | bytes 14680064 | tf_op jit(solution)/shard_map/reshape | solution.py:74
  171.7 199.3 %gather_fusion = f32[14336]{0:T(1024)S(1)} fusion(f32[14,32,4096]{2,1,0:T(8,128)} %reshape.93, s32[14336]{0:T(1024)S(1)} %reshape.103), kind=kCustom, calls=%fused_computation | custom fusion | bytes 286720 | tf_op jit(solution)/shard_map/jit(take_along_axis)/gather | solution.py:76
  371.4 78.6 %scatter_custom_fusion = f32[1835008]{0:T(1024)} fusion(s32[14336]{0:T(1024)S(1)} %reshape.109, f32[14336]{0:T(1024)S(1)} %reshape.111, f32[]{:T(128)} %constant.15.clone.1), kind=kCustom, calls=%fused_computation.11 | custom fusion | flops 14336 | bytes 7340036
  450.0 11.5 reshape.94
  461.5 18.2 %fusion.6 = f32[14,32,64,64]{2,3,1,0:T(8,128)S(1)} fusion(f32[14,32,64,64]{3,2,1,0:T(8,128)} %reshape.94, f32[64]{0:T(128)S(1)} %get-tuple-element.11, f32[64]{0:T(128)S(1)} %get-tuple-element.10), kind=kOutput, calls=%fused_computation.23 | convolution fusion | flops 1409298432 | bytes 14680576 | tf_op jit(solution)/shard_map/ui,pquv,vj->piqj/dot_general | solution.py:50
  479.7 14.6 %convolution_bitcast_fusion = f32[14,64,32,64]{3,1,2,0:T(8,128)} fusion(f32[14,32,64,64]{2,3,1,0:T(8,128)S(1)} %fusion.6, f32[64]{0:T(128)S(1)} %get-tuple-element.11, f32[64]{0:T(128)S(1)} %get-tuple-element.10), kind=kOutput, calls=%fused_computation.6 | convolution fusion | flops 1409298432 | bytes 14680576 | tf_op jit(solution)/shard_map/ui,pquv,vj->piqj/dot_general | solution.py:50
  494.4 21.3 %copy.34 = f32[14,64,32,64]{3,2,1,0:T(8,128)} copy(f32[14,64,32,64]{3,1,2,0:T(8,128)} %convolution_bitcast_fusion) | data formatting | bytes 14680064 | tf_op jit(solution)/shard_map/ui,pquv,vj->piqj/transpose | solution.py:50
  515.7 13.5 %all_gather_reshape.3 = f32[1,896,2048]{2,1,0:T(8,128)} reshape(f32[14,64,32,64]{3,2,1,0:T(8,128)} %copy.34) | data formatting | bytes 14680064 | tf_op jit(solution)/shard_map/all_gather;reshape | solution.py:80
  529.2 562.8 %all-gather.2.cloned.1.call-done = f32[8,896,2048]{2,1,0:T(8,128)} async-done(((f32[1,896,2048]{2,1,0:T(8,128)}), f32[8,896,2048]{2,1,0:T(8,128)}) %all-gather.2.cloned.1.call-update) | async-done | bytes 58720272 | tf_op jit(solution)/shard_map/all_gather | solution.py:80
  1092.0 21.8 %reduce_sum.9 = f32[896,2048]{1,0:T(8,128)} reduce(f32[8,896,2048]{2,1,0:T(8,128)} %all-gather.2.cloned.1.call-done, f32[]{:T(128)} %constant.15.clone.1), dimensions={0}, to_apply=%region_1.2 | reduce | flops 12845056 | bytes 66060292 | tf_op jit(solution)/shard_map/reduce_sum | solution.py:80
  1113.8 8.6 copy.36
  1122.3 8.1 fusion.27
  1130.4 5.3 copy.37
  1135.7 7.3 all-to-all-start.2
  1143.0 5.3 copy.38
  1148.3 40.0 %all-to-all-done.2 = f32[16,1,448,128]{3,2,1,0:T(8,128)} async-done(((f32[16,1,448,128]{3,2,1,0:T(8,128)}), f32[16,1,448,128]{3,2,1,0:T(8,128)}, u32[]{:S(2)}, u32[]{:S(2)}) %all-to-all-start.2) | async-done | bytes 3670048 | tf_op jit(solution)/shard_map/all_to_all | solution.py:34
  1188.3 5.3 all-to-all-start.3
  1193.6 13.2 %reshape.95 = f32[1,1,896,2048]{3,2,1,0:T(8,128)} reshape(f32[14,64,32,64]{3,2,1,0:T(8,128)} %copy.34) | data formatting | bytes 14680064 | tf_op jit(solution)/shard_map/reshape | solution.py:78
  1206.8 13.0 %fusion.2 = f32[1,1,896,2048]{3,2,1,0:T(8,128)} fusion(f32[1,1,896,2048]{3,2,1,0:T(8,128)} %reshape.95, f32[16,1,1,112,8,128]{5,4,3,2,1,0:T(8,128)} %get-tuple-element.4, f32[1,1,896,2048]{3,2,1,0:T(8,128)} %param.4), kind=kLoop, calls=%fused_computation.8 | loop fusion | flops 5505024 | bytes 29360128 | tf_op jit(solution)/shard_map/sub | solution.py:79
  1219.8 19.2 %all-to-all-done.3 = f32[16,1,448,128]{3,2,1,0:T(8,128)} async-done(((f32[16,1,448,128]{3,2,1,0:T(8,128)}), f32[16,1,448,128]{3,2,1,0:T(8,128)}, u32[]{:S(2)}, u32[]{:S(2)}) %all-to-all-start.3) | async-done | bytes 3670048 | tf_op jit(solution)/shard_map/all_to_all | solution.py:34
  1239.0 7.0 pad_maximum_fusion
  (25 shorter events, 9.8 us)
Async XLA Ops:
  7.2 43.6 %copy-start = (s32[14,32,8,32]{3,2,1,0:T(8,128)S(1)}, s32[14,32,8,32]{3,2,1,0:T(8,128)}, u32[]{:S(2)}) copy-start(s32[14,32,8,32]{3,2,1,0:T(8,128)} %param.5) | copy-start | bytes 1376260
  7.2 44.1 %copy-start.3 = (s32[3]{0:T(128)S(1)}, s32[3]{0:T(128)}, u32[]{:S(2)}) copy-start(s32[3]{0:T(128)} %constant.55) | copy-start | bytes 40
  7.2 44.2 %copy-start.2 = (s32[3]{0:T(128)S(1)}, s32[3]{0:T(128)}, u32[]{:S(2)}) copy-start(s32[3]{0:T(128)} %constant.58) | copy-start | bytes 40
  11.5 34.1 %all-to-all-start = ((bf16[16,1,1,448,128]{4,3,2,1,0:T(8,128)(2,1)}), bf16[16,1,1,448,128]{4,3,2,1,0:T(8,128)(2,1)}, u32[]{:S(2)}, u32[]{:S(2)}) async-start(bf16[16,1,1,448,128]{4,3,2,1,0:T(8,128)(2,1)} %get-tuple-element.6), calls=%async_computation | async-start | bytes 3670016 | tf_op jit(solution)/shard_map/all_to_all | solution.py:34
  45.5 30.9 %all-to-all-start.1 = ((bf16[16,1,1,448,128]{4,3,2,1,0:T(8,128)(2,1)}), bf16[16,1,1,448,128]{4,3,2,1,0:T(8,128)(2,1)}, u32[]{:S(2)}, u32[]{:S(2)}) async-start(bf16[16,1,1,448,128]{4,3,2,1,0:T(8,128)(2,1)} %get-tuple-element.7), calls=%async_computation.1 | async-start | bytes 3670016 | tf_op jit(solution)/shard_map/all_to_all | solution.py:34
  50.7 1041.2 %all-gather.2.cloned.1.call-start = ((), (), s32[]{:S(2)}) async-start(), calls=%async_computation.4 | async-start | bytes 66060288 | tf_op jit(solution)/shard_map/all_gather | solution.py:80
  1135.7 52.6 %all-to-all-start.2 = ((f32[16,1,448,128]{3,2,1,0:T(8,128)}), f32[16,1,448,128]{3,2,1,0:T(8,128)}, u32[]{:S(2)}, u32[]{:S(2)}) async-start(f32[16,1,448,128]{3,2,1,0:T(8,128)} %copy.37), calls=%async_computation.2 | async-start | bytes 7340032 | tf_op jit(solution)/shard_map/all_to_all | solution.py:34
  1188.3 50.7 %all-to-all-start.3 = ((f32[16,1,448,128]{3,2,1,0:T(8,128)}), f32[16,1,448,128]{3,2,1,0:T(8,128)}, u32[]{:S(2)}, u32[]{:S(2)}) async-start(f32[16,1,448,128]{3,2,1,0:T(8,128)} %copy.38), calls=%async_computation.3 | async-start | bytes 7340032 | tf_op jit(solution)/shard_map/all_to_all | solution.py:34
  1239.0 7.0 copy-start.1
Sparse Core Ops, SparseCore 0:
  529.3 562.5 all-gather.1
